TPU v7x, 32 devices: a whole 2x2x4 slice. The times are simulated.
32 devices in a mesh: rep: 8 (over z, core), tp: 4 (over y, x).
Axes of the slice: x: 2, y: 2, z: 4, core: 2. Of those that a mesh axis runs over, the one named last changes fastest.
Arguments:
- hidden_state: bfloat16 [32, 3584], P('rep'), may hold values from -6 to 6
- lengths: int32 [32], P('rep'), may hold values from 1 to 2048, as said below
- old_qkv: bfloat16 [3584, 4608], P(None, 'tp'), may hold values from -0.09375 to 0.09375
- old_out: bfloat16 [3584, 3584], P(None, 'tp'), may hold values from -0.09375 to 0.09375
- cache_keys: bfloat16 [32, 2048, 512], P('rep', 'tp'), may hold values from -64 to 64
- cache_values: bfloat16 [32, 2048, 512], P('rep', 'tp'), may hold values from -6 to 6
- new_qkv: bfloat16 [3584, 4608], P(('rep', 'tp')), may hold values from -0.09375 to 0.09375
- new_out: bfloat16 [3584, 3584], P(('rep', 'tp')), may hold values from -0.09375 to 0.09375
Outputs:
- decoded: bfloat16 [32, 3584], P('rep', 'tp')
- resharded_qkv: bfloat16 [3584, 4608], P(None, 'tp')
- resharded_out: bfloat16 [3584, 3584], P(None, 'tp')
Inputs may be any that keep to these rules, and one draw needn't show every extreme that they name: Every sequence has 1 to 2048 cached tokens, held in positions 0 to lengths - 1; in every draw some sequence fills its cache.
All inputs are finite; a program needn't handle non-finite values.
Results may differ from a plain program's by a relative error of at most 0.012.
Values may be sent and summed in bfloat16 or wider, within the bound.
No kernel may reach another device: no remote copies, remote signals or barrier semaphores. Data moves between devices by JAX's collectives and lax.ppermute only.
A program may use at most 128 MiB of HBM per device.

v0:
```python
import jax
import jax.numpy as jnp
from jax import lax
from jax.sharding import PartitionSpec as P

HQ = 28
KVH = 4
HD = 128


ROPE_BASE = 1000000.0


def rotate(vectors, positions):
    half_dim = vectors.shape[-1] // 2
    frequency = ROPE_BASE ** (-2.0 * jnp.arange(half_dim, dtype=jnp.float32) / (2 * half_dim))
    angles = positions.astype(jnp.float32)[:, None, None] * frequency
    first_half = vectors[..., :half_dim]
    second_half = vectors[..., half_dim:]
    return jnp.concatenate(
        [
            first_half * jnp.cos(angles) - second_half * jnp.sin(angles),
            second_half * jnp.cos(angles) + first_half * jnp.sin(angles),
        ],
        axis=-1,
    )


def per_device(hidden_state, lengths, old_qkv, old_out, cache_keys, cache_values, new_qkv, new_out):
    pieces = (
        lax.all_to_all(new_qkv, "tp", split_axis=1, concat_axis=0, tiled=True),
        lax.all_to_all(new_out, "tp", split_axis=1, concat_axis=0, tiled=True),
    )
    qkv_tp, out_tp = (
        lax.all_gather(pieces[0], "rep", axis=0, tiled=True),
        lax.all_gather(pieces[1], "rep", axis=0, tiled=True),
    )
    seq_count = hidden_state.shape[0]
    local_joined = jnp.dot(hidden_state, old_qkv, preferred_element_type=jnp.float32).astype(
        jnp.bfloat16
    )
    joined_rows = lax.all_gather(local_joined, "tp", axis=1, tiled=True)
    q_width = HQ * HD
    k_width = KVH * HD
    group_size = HQ // KVH
    queries = rotate(
        joined_rows[:, :q_width].astype(jnp.float32).reshape(seq_count, HQ, HD), lengths
    ).astype(jnp.bfloat16)
    own_keys = rotate(
        joined_rows[:, q_width : q_width + k_width].astype(jnp.float32).reshape(seq_count, KVH, HD),
        lengths,
    ).astype(jnp.bfloat16)
    own_values = joined_rows[:, q_width + k_width :].reshape(seq_count, KVH, HD)
    inv_root = 1.0 / jnp.sqrt(jnp.float32(HD))
    cache_rows = cache_keys.shape[1]
    grouped = queries.reshape(seq_count, KVH, group_size, HD)
    key_blocks = cache_keys.reshape(seq_count, cache_rows, KVH, HD)
    value_blocks = cache_values.reshape(seq_count, cache_rows, KVH, HD)
    scores = (
        jnp.einsum("skgd,stkd->skgt", grouped, key_blocks, preferred_element_type=jnp.float32)
        * inv_root
    )
    positions = lax.axis_index("tp") * cache_rows + jnp.arange(cache_rows, dtype=jnp.int32)
    live_mask = (positions[None, :] < lengths[:, None])[:, None, None, :]
    scores = jnp.where(live_mask, scores, jnp.float32(-1e30))
    own_score = (
        jnp.sum(grouped.astype(jnp.float32) * own_keys.astype(jnp.float32)[:, :, None, :], axis=-1)
        * inv_root
    )
    local_top = jnp.maximum(jnp.max(scores, axis=-1), own_score)
    top_score = lax.pmax(local_top, "tp")
    weights = jnp.where(live_mask, jnp.exp(scores - top_score[..., None]), jnp.float32(0.0)).astype(
        jnp.bfloat16
    )
    numer_part = jnp.einsum(
        "skgt,stkd->skgd", weights, value_blocks, preferred_element_type=jnp.float32
    )
    denom_part = jnp.sum(weights.astype(jnp.float32), axis=-1)
    numerator, denominator = lax.psum((numer_part, denom_part), "tp")
    own_weight = lax.optimization_barrier(
        jnp.exp(own_score - top_score).astype(jnp.bfloat16)
    ).astype(jnp.float32)
    numerator = numerator + own_weight[..., None] * own_values.astype(jnp.float32)[:, :, None, :]
    denominator = denominator + own_weight
    attended = (numerator / denominator[..., None]).reshape(seq_count, q_width).astype(jnp.bfloat16)
    decoded = jnp.dot(attended, old_out, preferred_element_type=jnp.float32).astype(jnp.bfloat16)
    return (decoded, qkv_tp, out_tp)


def solution(mesh):
    in_specs = (
        P("rep", None),
        P("rep"),
        P(None, "tp"),
        P(None, "tp"),
        P("rep", "tp", None),
        P("rep", "tp", None),
        P(("rep", "tp"), None),
        P(("rep", "tp"), None),
    )
    out_specs = (P("rep", "tp"), P(None, "tp"), P(None, "tp"))
    return jax.shard_map(
        per_device, mesh=mesh, in_specs=in_specs, out_specs=out_specs, check_vma=False
    )
```

profile of v0, /device:TPU:0, one launch (start us, length us, event | category | flops | bytes accessed | tf_op | source)
XLA Modules:
  0.0 192.4 jit_solution(7465929102253558879)
XLA Ops:
  7.2 0.0 copy-start
  7.2 0.0 copy-start.1
  7.2 0.0 all-gather.5.cloned.1.call-start
  7.2 1.4 copy.44
  8.6 16.9 %all_to_all.38 = bf16[112,4,896]{2,0,1:T(8,128)(2,1)} all-to-all(bf16[112,4,896]{2,0,1:T(8,128)(2,1)S(1)} %bitcast.46), channel_id=1, replica_groups=mesh['rep'=8,'tp'=4] {'tp'}, dimensions={1} | all-to-all | bytes 1605632 | tf_op jit(solution)/shard_map/all_to_all | solution.py:32
  25.5 0.0 all-gather.5.cloned.1.call-update
  25.6 0.0 all-gather.3.cloned.1.call-start
  25.6 0.0 copy-start.2
  25.6 0.1 copy.43
  25.7 16.3 %all_to_all.39 = bf16[112,4,1152]{2,0,1:T(8,128)(2,1)} all-to-all(bf16[112,4,1152]{2,0,1:T(8,128)(2,1)S(1)} %bitcast.44), channel_id=1, replica_groups=mesh['rep'=8,'tp'=4] {'tp'}, dimensions={1} | all-to-all | bytes 2064384 | tf_op jit(solution)/shard_map/all_to_all | solution.py:31
  42.0 0.0 all-gather.3.cloned.1.call-update
  42.0 0.0 copy-start.3
  42.0 4.6 %convolution_convert_fusion = bf16[4,1152]{1,0:T(4,128)(2,1)S(1)} fusion(bf16[4,3584]{1,0:T(4,128)(2,1)S(1)} %copy-done.2, bf16[3584,1152]{1,0:T(8,128)(2,1)} %param.10), kind=kOutput, calls=%fused_computation | convolution fusion | flops 33034752 | bytes 8295424 | tf_op jit(solution)/shard_map/dot_general | solution.py:39
  46.7 7.6 %all_gather.9 = bf16[4,4608]{1,0:T(4,128)(2,1)S(1)} all-gather(bf16[4,1152]{1,0:T(4,128)(2,1)S(1)} %convolution_convert_fusion), channel_id=1, replica_groups=mesh['rep'=8,'tp'=4] {'tp'}, dimensions={1}, use_global_device_ids=true | all-gather | bytes 46080 | tf_op jit(solution)/shard_map/all_gather | solution.py:42
  54.4 0.1 multiply_cosine_fusion
  54.5 0.1 subtract_convert_fusion
  54.7 0.1 subtract_convert_fusion.1
  54.7 0.1 maximum_convert_fusion
  54.8 0.2 multiply_reduce_fusion
  55.0 0.1 broadcast_compare_fusion
  55.1 0.0 copy-done
  55.1 0.8 fusion.14
  55.9 9.1 %pmax.7 = f32[4,4,7]{2,1,0:T(4,128)S(1)} all-reduce(f32[4,4,7]{2,1,0:T(4,128)S(1)} %multiply_maximum_fusion), channel_id=1, replica_groups=mesh['rep'=8,'tp'=4] {'tp'}, use_global_device_ids=true, to_apply=%region_2.3 | all-reduce | flops 112 | bytes 896 | tf_op jit(solution)/shard_map/pmax | solution.py:71
  65.0 0.2 convert_reduce_fusion
  65.2 2.1 %fusion = f32[4,4,7,128]{3,2,1,0:T(8,128)S(1)} fusion(f32[4,4,7,512]{3,2,1,0:T(8,128)S(1)} %get-tuple-element.14, f32[4,4,7]{2,1,0:T(4,128)S(1)} %pmax.7, pred[4,512]{1,0:T(4,128)(4,1)S(1)} %broadcast_compare_fusion, bf16[4,512,512]{2,1,0:T(8,128)(2,1)} %param.13), kind=kOutput, calls=%fused_computation.1 | convolution fusion | flops 14852096 | bytes 2386368 | tf_op jit(solution)/shard_map/skgt,stkd->skgd/dot_general | solution.py:75
  67.3 16.0 %all-reduce = (f32[4,4,7,128]{3,2,1,0:T(8,128)S(1)}, f32[4,4,7]{2,1,0:T(4,128)S(1)}) all-reduce(f32[4,4,7,128]{3,2,1,0:T(8,128)S(1)} %fusion, f32[4,4,7]{2,1,0:T(4,128)S(1)} %convert_reduce_fusion), channel_id=1, replica_groups=mesh['rep'=8,'tp'=4] {'tp'}, use_global_device_ids=true, to_apply=%region_3.4 | all-reduce | flops 14448 | bytes 115584 | tf_op jit(solution)/shard_map/psum | solution.py:79
  83.3 0.1 divide_convert_fusion
  83.4 4.4 %convolution_convert_fusion.1 = bf16[4,896]{1,0:T(4,128)(2,1)} fusion(bf16[4,3584]{1,0:T(4,128)(2,1)S(1)} %convert_element_type.68, bf16[3584,896]{1,0:T(8,128)(2,1)} %param.11), kind=kOutput, calls=%fused_computation.9 | convolution fusion | flops 25693696 | bytes 6458368 | tf_op jit(solution)/shard_map/dot_general | solution.py:86
  87.8 3.1 %all-gather.5.cloned.1.call-done = bf16[3584,896]{1,0:T(8,128)(2,1)} async-done(((bf16[448,896]{1,0:T(8,128)(2,1)}), bf16[3584,896]{1,0:T(8,128)(2,1)}) %all-gather.5.cloned.1.call-update) | async-done | bytes 6422544 | tf_op jit(solution)/shard_map/all_gather | solution.py:36
  90.9 81.3 %all-gather.3.cloned.1.call-done = bf16[3584,1152]{1,0:T(8,128)(2,1)} async-done(((bf16[448,1152]{1,0:T(8,128)(2,1)}), bf16[3584,1152]{1,0:T(8,128)(2,1)}) %all-gather.3.cloned.1.call-update) | async-done | bytes 8257552 | tf_op jit(solution)/shard_map/all_gather | solution.py:35
  172.2 7.3 %copy.47 = bf16[3584,1152]{1,0:T(8,128)(2,1)} copy(bf16[3584,1152]{1,0:T(8,128)(2,1)} %all-gather.3.cloned.1.call-done) | data formatting | bytes 16515072
  179.5 6.1 %copy.48 = bf16[3584,896]{1,0:T(8,128)(2,1)} copy(bf16[3584,896]{1,0:T(8,128)(2,1)} %all-gather.5.cloned.1.call-done) | data formatting | bytes 12845056
  (20 shorter events, 0.2 us)
Async XLA Ops:
  7.2 47.9 %copy-start = (bf16[4,512,512]{2,1,0:T(8,128)(2,1)S(1)}, bf16[4,512,512]{2,1,0:T(8,128)(2,1)}, u32[]{:S(2)}) copy-start(bf16[4,512,512]{2,1,0:T(8,128)(2,1)} %param.12) | copy-start | bytes 6291460
  7.2 18.4 %copy-start.1 = (bf16[112,4608]{1,0:T(8,128)(2,1)S(1)}, bf16[112,4608]{1,0:T(8,128)(2,1)}, u32[]{:S(2)}) copy-start(bf16[112,4608]{1,0:T(8,128)(2,1)} %param.14) | copy-start | bytes 3096580
  7.2 83.7 %all-gather.5.cloned.1.call-start = ((), (), s32[]{:S(2)}) async-start(), calls=%async_computation.3 | async-start | bytes 7225344 | tf_op jit(solution)/shard_map/all_gather | solution.py:36
  25.6 146.6 %all-gather.3.cloned.1.call-start = ((), (), s32[]{:S(2)}) async-start(), calls=%async_computation.2 | async-start | bytes 9289728 | tf_op jit(solution)/shard_map/all_gather | solution.py:35
  25.6 16.4 %copy-start.2 = (bf16[4,3584]{1,0:T(4,128)(2,1)S(1)}, bf16[4,3584]{1,0:T(4,128)(2,1)}, u32[]{:S(2)}) copy-start(bf16[4,3584]{1,0:T(4,128)(2,1)} %param.8) | copy-start | bytes 86020
  42.0 12.2 %copy-start.3 = (s32[4]{0:T(128)S(1)}, s32[4]{0:T(128)}, u32[]{:S(2)}) copy-start(s32[4]{0:T(128)} %param.9) | copy-start | bytes 52
Sparse Core Ops, SparseCore 0:
  25.7 65.1 all-gather.4
  92.5 79.5 all-gather.2
where the time goes:
time: 193 us; the launch traced here: 192 us
  waiting for transfers between devices  84.4 us (44%)
  blocking collectives  65.8 us (34%)
  local copies, waits for them, and re-layouts  15 us (8%)
  between operations  14.2 us (7%)
  matrix products  11.9 us (6%)
    all_gather x1, waiting for transfers between devices, per_device(): lax.all_gather(pieces[0], 'rep', axis=0, tiled=True)  81.3 us
    all_to_all x1, blocking collectives, per_device(): lax.all_to_all(new_out, 'tp', split_axis=1, concat_axis=0, tiled=True)  16.9 us
    all_to_all x1, blocking collectives, per_device(): lax.all_to_all(new_qkv, 'tp', split_axis=1, concat_axis=0, tiled=True)  16.3 us
    psum x1, blocking collectives, per_device(): numerator, denominator = lax.psum((numer_part, denom_part), 'tp')  16 us
    unnamed x10, local copies, waits for them, and re-layouts  13.4 us
    pmax x1, blocking collectives, per_device(): top_score = lax.pmax(local_top, 'tp')  9.08 us
    all_gather x1, blocking collectives, per_device(): joined_rows = lax.all_gather(local_joined, 'tp', axis=1, tiled=True)  7.56 us
    dot_general x1, matrix products, per_device(): jnp.dot(hidden_state, old_qkv, preferred_element_type=jnp.float32)  4.65 us
  transfers between devices with their start and end apart: 2, of which 2 were waited for; matrix products, arithmetic and copies ran while one was open for 7% of the time, Pallas kernels for 0%

commit v1 on v0

--- a/solution.py
+++ b/solution.py
@@ -1,12 +1,16 @@
 import jax
 import jax.numpy as jnp
 from jax import lax
+from jax.experimental import pallas as pl
+from jax.experimental.pallas import tpu as pltpu
+from jax.sharding import Mesh
 from jax.sharding import PartitionSpec as P
+
 
 HQ = 28
 KVH = 4
 HD = 128
-
+CORES = 2
 
 ROPE_BASE = 1000000.0
 
@@ -26,15 +30,116 @@
     )
 
 
-def per_device(hidden_state, lengths, old_qkv, old_out, cache_keys, cache_values, new_qkv, new_out):
-    pieces = (
-        lax.all_to_all(new_qkv, "tp", split_axis=1, concat_axis=0, tiled=True),
-        lax.all_to_all(new_out, "tp", split_axis=1, concat_axis=0, tiled=True),
-    )
-    qkv_tp, out_tp = (
-        lax.all_gather(pieces[0], "rep", axis=0, tiled=True),
-        lax.all_gather(pieces[1], "rep", axis=0, tiled=True),
-    )
+def place_pieces(device, pieces, row_of, outs, widths, total_rows):
+    count = len(pieces)
+    height = pieces[0].shape[0]
+    aliased = 0 if outs is None else len(outs)
+
+    def kernel(device_ref, *refs):
+        piece_refs = refs[:count]
+        out_refs = refs[count + aliased : count + aliased + len(widths)]
+        sem = refs[-1]
+        copies = []
+        for at, piece in enumerate(piece_refs):
+            first = pl.multiple_of(row_of[at](device_ref[0]), 16)
+            column = 0
+            for out_at, (out, width) in enumerate(zip(out_refs, widths)):
+                copies.append(
+                    pltpu.make_async_copy(
+                        piece.at[:, pl.ds(column, width)],
+                        out.at[pl.ds(first, height), :],
+                        sem.at[at, out_at],
+                    )
+                )
+                column += width
+        for copy in copies:
+            copy.start()
+        for copy in copies:
+            copy.wait()
+
+    dtype = pieces[0].dtype
+    return pl.pallas_call(
+        kernel,
+        out_shape=[jax.ShapeDtypeStruct((total_rows, width), dtype) for width in widths],
+        in_specs=[pl.BlockSpec(memory_space=pltpu.SMEM)]
+        + [pl.BlockSpec(memory_space=pl.ANY)] * (count + aliased),
+        out_specs=[pl.BlockSpec(memory_space=pl.ANY)] * len(widths),
+        scratch_shapes=[pltpu.SemaphoreType.DMA((count, len(widths)))],
+        input_output_aliases={1 + count + at: at for at in range(aliased)},
+    )(device, *pieces, *(() if outs is None else outs))
+
+
+def reshard_by_permutes(new_qkv, new_out, outer, tp):
+    height = new_qkv.shape[0]
+    widths = (new_qkv.shape[1] // tp, new_out.shape[1] // tp)
+    t = lax.axis_index("tp")
+    device = lax.axis_index(("outer", "core", "tp")).astype(jnp.int32).reshape(1)
+    ring = [(i, (i + 1) % outer) for i in range(outer)]
+    swap = [(i, i ^ 1) for i in range(CORES)]
+
+    def columns_for(peer):
+        return jnp.concatenate(
+            [
+                lax.dynamic_slice_in_dim(array, peer * width, width, 1)
+                for array, width in zip((new_qkv, new_out), widths)
+            ],
+            axis=1,
+        )
+
+    mine = {}
+    for j in range(tp):
+        mine[0, j] = columns_for(t ^ j)
+        if j:
+            mine[0, j] = lax.ppermute(mine[0, j], "tp", [(i, i ^ j) for i in range(tp)])
+    for s in range(1, outer):
+        for j in range(tp):
+            mine[s, j] = lax.ppermute(mine[s - 1, j], "outer", ring)
+    theirs = {}
+    for at, piece in mine.items():
+        theirs[at] = lax.ppermute(piece, "core", swap)
+
+    def row_of(at, other):
+        def rows(device):
+            z = device // (CORES * tp)
+            c = device // tp % CORES
+            z = (z - at[0] + outer) % outer
+            c = 1 - c if other else c
+            return ((z * CORES + c) * tp + (device % tp ^ at[1])) * height
+
+        return rows
+
+    outs = None
+    for group in place_groups(outer, tp):
+        pieces = [mine[at] for at in group] + [theirs[at] for at in group]
+        rows = [row_of(at, False) for at in group] + [row_of(at, True) for at in group]
+        outs = place_pieces(device, pieces, rows, outs, widths, height * outer * CORES * tp)
+    return tuple(outs)
+
+
+def place_groups(outer, tp):
+    blocks = [(s, j) for s in range(outer) for j in range(tp)]
+    last = blocks[-1:]
+    return [
+        [at for at in blocks if at[0] < outer - 2],
+        [at for at in blocks if at[0] == outer - 2],
+        [at for at in blocks if at[0] == outer - 1 and at not in last],
+        last,
+    ]
+
+
+def reshard_by_collectives(new_qkv, new_out):
+    return tuple(
+        lax.all_gather(
+            lax.all_to_all(array, "tp", split_axis=1, concat_axis=0, tiled=True),
+            ("outer", "core"),
+            axis=0,
+            tiled=True,
+        )
+        for array in (new_qkv, new_out)
+    )
+
+
+def decode(hidden_state, lengths, old_qkv, old_out, cache_keys, cache_values):
     seq_count = hidden_state.shape[0]
     local_joined = jnp.dot(hidden_state, old_qkv, preferred_element_type=jnp.float32).astype(
         jnp.bfloat16
@@ -83,22 +188,46 @@
     numerator = numerator + own_weight[..., None] * own_values.astype(jnp.float32)[:, :, None, :]
     denominator = denominator + own_weight
     attended = (numerator / denominator[..., None]).reshape(seq_count, q_width).astype(jnp.bfloat16)
-    decoded = jnp.dot(attended, old_out, preferred_element_type=jnp.float32).astype(jnp.bfloat16)
-    return (decoded, qkv_tp, out_tp)
+    return jnp.dot(attended, old_out, preferred_element_type=jnp.float32).astype(jnp.bfloat16)
 
 
 def solution(mesh):
+    rep, tp = mesh.shape["rep"], mesh.shape["tp"]
+    outer = rep // CORES
+    split = Mesh(mesh.devices.reshape(outer, CORES, tp), ("outer", "core", "tp"))
+    rep_axes = ("outer", "core")
+
+    def by_permutes(hidden_state, lengths, old_qkv, old_out, cache_keys, cache_values, new_qkv, new_out):
+        weights = reshard_by_permutes(new_qkv, new_out, outer, tp)
+        decoded = decode(hidden_state, lengths, old_qkv, old_out, cache_keys, cache_values)
+        return (decoded, *weights)
+
+    def by_collectives(hidden_state, lengths, old_qkv, old_out, cache_keys, cache_values, new_qkv, new_out):
+        weights = reshard_by_collectives(new_qkv, new_out)
+        decoded = decode(hidden_state, lengths, old_qkv, old_out, cache_keys, cache_values)
+        return (decoded, *weights)
+
     in_specs = (
-        P("rep", None),
-        P("rep"),
+        P(rep_axes, None),
+        P(rep_axes),
         P(None, "tp"),
         P(None, "tp"),
-        P("rep", "tp", None),
-        P("rep", "tp", None),
-        P(("rep", "tp"), None),
-        P(("rep", "tp"), None),
-    )
-    out_specs = (P("rep", "tp"), P(None, "tp"), P(None, "tp"))
-    return jax.shard_map(
-        per_device, mesh=mesh, in_specs=in_specs, out_specs=out_specs, check_vma=False
-    )
+        P(rep_axes, "tp", None),
+        P(rep_axes, "tp", None),
+        P((*rep_axes, "tp"), None),
+        P((*rep_axes, "tp"), None),
+    )
+    out_specs = (P(rep_axes, "tp"), P(None, "tp"), P(None, "tp"))
+
+    def step(*args):
+        new_qkv, new_out = args[-2:]
+        height = new_qkv.shape[0] // (rep * tp)
+        widths = (new_qkv.shape[1] // tp, new_out.shape[1] // tp)
+        pieced = height % 16 == 0 and all(width % 128 == 0 for width in widths)
+        body = by_permutes if pieced and outer >= 4 else by_collectives
+        run = jax.shard_map(
+            body, mesh=split, in_specs=in_specs, out_specs=out_specs, check_vma=False
+        )
+        return run(*args)
+
+    return step

time: 193 us -> 603 us (3.12)
  Pallas kernels: 0 us -> 450 us
  blocking collectives: 65.8 us -> 44 us
  starting transfers between devices: 0.08 us -> 14 us
  between operations: 14.2 us -> 1.12 us
  local copies, waits for them, and re-layouts: 15 us -> 3.36 us
  waiting for transfers between devices: 84.4 us -> 77.1 us
    pallas_call x0 -> x4, Pallas kernels: none -> 450 us  [place_pieces(): pl.pallas_call(kernel, out_shape=[jax.ShapeDtypeStruct((total_rows, width...]
    all_gather x2 -> x0, waiting for transfers between devices: 84.4 us -> none  [the longest x1 81.3 us: per_device(): lax.all_gather(pieces[0], 'rep', axis=0, tiled=True)]
    ppermute x0 -> x31, waiting for transfers between devices: none -> 77.1 us  [the longest x12 77 us: reshard_by_permutes(): mine[s, j] = lax.ppermute(mine[s - 1, j], 'outer', ring)]
    all_to_all x2 -> x0, blocking collectives: 33.2 us -> none  [the longest x1 16.9 us: per_device(): lax.all_to_all(new_out, 'tp', split_axis=1, concat_axis=0, tiled=True)]
    ppermute x0 -> x31, starting transfers between devices: none -> 14 us  [the longest x12 8.65 us: reshard_by_permutes(): mine[s, j] = lax.ppermute(mine[s - 1, j], 'outer', ring)]
    unnamed x10 -> x20, local copies, waits for them, and re-layouts: 13.4 us -> 0.36 us
    all_gather x1, blocking collectives: 7.56 us -> 18.6 us  [decode(): joined_rows = lax.all_gather(local_joined, 'tp', axis=1, tiled=True)]
  transfers between devices with their start and end apart: 2 -> 31, of which waited for: 2 -> 9; matrix products, arithmetic and copies ran while one was open for 7% -> 2% of each run, Pallas kernels for 0% -> 70%
where the time goes in v1:
time: 603 us
  Pallas kernels  450 us (75%)
  waiting for transfers between devices  77.1 us (13%)
  blocking collectives  44 us (7%)
  starting transfers between devices  14 us (2%)
  matrix products  11.7 us (2%)
    pallas_call x4, Pallas kernels, place_pieces(): pl.pallas_call(kernel, out_shape=[jax.ShapeDtypeStruct((total_rows, width...  450 us
    ppermute x12, waiting for transfers between devices, reshard_by_permutes(): mine[s, j] = lax.ppermute(mine[s - 1, j], 'outer', ring)  77 us
    all_gather x1, blocking collectives, decode(): joined_rows = lax.all_gather(local_joined, 'tp', axis=1, tiled=True)  18.6 us
    psum x1, blocking collectives, decode(): numerator, denominator = lax.psum((numer_part, denom_part), 'tp')  16.3 us
  transfers between devices with their start and end apart: 31, of which 9 were waited for; matrix products, arithmetic and copies ran while one was open for 2% of the time, Pallas kernels for 70%

profile of v1, /device:TPU:0, one launch (start us, length us, event | category | flops | bytes accessed | tf_op | source)
XLA Modules:
  0.0 602.8 jit_solution(11033182262002652784)
XLA Ops:
  0.7 1.5 constant_dynamic-slice_fusion.1
  2.2 1.3 constant_dynamic-slice_fusion
  3.6 3.1 collective-permute-start.5
  6.8 1.6 collective-permute-start.8
  8.4 1.6 collective-permute-start.12
  10.0 0.8 pad_maximum_fusion
  11.3 4.5 convolution_convert_fusion
  15.8 18.6 %all_gather.3 = bf16[4,4608]{1,0:T(4,128)(2,1)S(1)} all-gather(bf16[4,1152]{1,0:T(4,128)(2,1)S(1)} %convolution_convert_fusion), channel_id=1, replica_groups=mesh['outer'=4,'core'=2,'tp'=4] {'tp'}, dimensions={1}, use_global_device_ids=true | all-gather | bytes 46080 | tf_op jit(solution)/shard_map/all_gather | solution.py:147
  34.5 1.6 collective-permute-start.9
  36.5 1.6 collective-permute-start.13
  38.6 11.4 %collective-permute-done.9.refs_5_ = bf16[112,2048]{1,0:T(8,128)(2,1)} collective-permute-done((bf16[112,2048]{1,0:T(8,128)(2,1)}, bf16[112,2048]{1,0:T(8,128)(2,1)}, u32[]{:S(2)}, u32[]{:S(2)}) %collective-permute-start.9) | collective-permute-done | bytes 458784 | tf_op jit(solution)/shard_map/ppermute | solution.py:96
  50.5 9.4 %collective-permute-done.13.refs_6_ = bf16[112,2048]{1,0:T(8,128)(2,1)} collective-permute-done((bf16[112,2048]{1,0:T(8,128)(2,1)}, bf16[112,2048]{1,0:T(8,128)(2,1)}, u32[]{:S(2)}, u32[]{:S(2)}) %collective-permute-start.13) | collective-permute-done | bytes 458784 | tf_op jit(solution)/shard_map/ppermute | solution.py:96
  59.9 7.4 %collective-permute-done.1.refs_7_ = bf16[112,2048]{1,0:T(8,128)(2,1)S(1)} collective-permute-done((bf16[112,2048]{1,0:T(8,128)(2,1)}, bf16[112,2048]{1,0:T(8,128)(2,1)S(1)}, u32[]{:S(2)}, u32[]{:S(2)}) %collective-permute-start.1) | collective-permute-done | bytes 458784 | tf_op jit(solution)/shard_map/ppermute | solution.py:96
  67.4 0.5 collective-permute-start.29
  68.1 0.8 fusion.14
  68.8 1.3 collective-permute-start.10
  70.1 12.7 %collective-permute-done.6.refs_0_ = bf16[112,2048]{1,0:T(8,128)(2,1)} collective-permute-done((bf16[112,2048]{1,0:T(8,128)(2,1)}, bf16[112,2048]{1,0:T(8,128)(2,1)}, u32[]{:S(2)}, u32[]{:S(2)}) %collective-permute-start.6) | collective-permute-done | bytes 458784 | tf_op jit(solution)/shard_map/ppermute | solution.py:96
  83.0 0.6 collective-permute-start.7
  83.9 9.1 %pmax.7 = f32[4,4,7]{2,1,0:T(4,128)S(1)} all-reduce(f32[4,4,7]{2,1,0:T(4,128)S(1)} %multiply_maximum_fusion), channel_id=1, replica_groups=mesh['outer'=4,'core'=2,'tp'=4] {'tp'}, use_global_device_ids=true, to_apply=%region_2.3 | all-reduce | flops 112 | bytes 896 | tf_op jit(solution)/shard_map/pmax | solution.py:176
  93.0 2.0 fusion
  95.1 7.4 %collective-permute-done.14.refs_2_ = bf16[112,2048]{1,0:T(8,128)(2,1)} collective-permute-done((bf16[112,2048]{1,0:T(8,128)(2,1)}, bf16[112,2048]{1,0:T(8,128)(2,1)}, u32[]{:S(2)}, u32[]{:S(2)}) %collective-permute-start.14) | collective-permute-done | bytes 458784 | tf_op jit(solution)/shard_map/ppermute | solution.py:96
  102.5 9.8 %collective-permute-done.2.refs_3_ = bf16[112,2048]{1,0:T(8,128)(2,1)} collective-permute-done((bf16[112,2048]{1,0:T(8,128)(2,1)S(1)}, bf16[112,2048]{1,0:T(8,128)(2,1)}, u32[]{:S(2)}, u32[]{:S(2)}) %collective-permute-start.2) | collective-permute-done | bytes 458784 | tf_op jit(solution)/shard_map/ppermute | solution.py:96
  112.3 9.8 %collective-permute-done.7.refs_0_ = bf16[112,2048]{1,0:T(8,128)(2,1)} collective-permute-done((bf16[112,2048]{1,0:T(8,128)(2,1)}, bf16[112,2048]{1,0:T(8,128)(2,1)}, u32[]{:S(2)}, u32[]{:S(2)}) %collective-permute-start.7) | collective-permute-done | bytes 458784 | tf_op jit(solution)/shard_map/ppermute | solution.py:96
  122.4 16.3 %all-reduce = (f32[4,4,7,128]{3,2,1,0:T(8,128)S(1)}, f32[4,4,7]{2,1,0:T(4,128)S(1)}) all-reduce(f32[4,4,7,128]{3,2,1,0:T(8,128)S(1)} %fusion, f32[4,4,7]{2,1,0:T(4,128)S(1)} %convert_reduce_fusion), channel_id=1, replica_groups=mesh['outer'=4,'core'=2,'tp'=4] {'tp'}, use_global_device_ids=true, to_apply=%region_3.4 | all-reduce | flops 14448 | bytes 115584 | tf_op jit(solution)/shard_map/psum | solution.py:184
  138.8 0.5 collective-permute-start.16
  139.4 2.4 collective-permute-done.15.refs_2_
  141.8 6.7 %collective-permute-done.3.refs_0_ = bf16[112,2048]{1,0:T(8,128)(2,1)} collective-permute-done((bf16[112,2048]{1,0:T(8,128)(2,1)}, bf16[112,2048]{1,0:T(8,128)(2,1)}, u32[]{:S(2)}, u32[]{:S(2)}) %collective-permute-start.3) | collective-permute-done | bytes 458784 | tf_op jit(solution)/shard_map/ppermute | solution.py:96
  148.6 4.4 convolution_convert_fusion.1
  153.0 223.7 %shard_map.103 = (bf16[3584,1152]{1,0:T(8,128)(2,1)}, bf16[3584,896]{1,0:T(8,128)(2,1)}) custom-call(s32[1]{0:T(128)} %bitcast.2.device_ref, bf16[112,2048]{1,0:T(8,128)(2,1)} %copy-done.1, bf16[112,2048]{1,0:T(8,128)(2,1)} %collective-permute-done.8.refs_1_, bf16[112,2048]{1,0:T(8,128)(2,1)} %collective-permute-done.12.refs_2_, ...), custom_call_target="tpu_custom_call" | custom-call | tf_op jit(solution)/shard_map/pallas_call | solution.py:61
  376.8 112.4 %shard_map.104 = (bf16[3584,1152]{1,0:T(8,128)(2,1)}, bf16[3584,896]{1,0:T(8,128)(2,1)}) custom-call(s32[1]{0:T(128)} %bitcast.2.device_ref, bf16[112,2048]{1,0:T(8,128)(2,1)} %collective-permute-done.6.refs_0_, bf16[112,2048]{1,0:T(8,128)(2,1)} %collective-permute-done.10.refs_1_, ...), custom_call_target="tpu_custom_call", output_to_operand_aliasing={{0}: (9, {}), {1}: (10, {})} | custom-call | tf_op jit(solution)/shard_map/pallas_call | solution.py:61
  489.3 84.6 %shard_map.105 = (bf16[3584,1152]{1,0:T(8,128)(2,1)}, bf16[3584,896]{1,0:T(8,128)(2,1)}) custom-call(s32[1]{0:T(128)} %bitcast.2.device_ref, bf16[112,2048]{1,0:T(8,128)(2,1)} %collective-permute-done.7.refs_0_, bf16[112,2048]{1,0:T(8,128)(2,1)} %collective-permute-done.11.refs_1_, ...), custom_call_target="tpu_custom_call", output_to_operand_aliasing={{0}: (7, {}), {1}: (8, {})} | custom-call | tf_op jit(solution)/shard_map/pallas_call | solution.py:61
  573.9 29.0 %shard_map.106 = (bf16[3584,1152]{1,0:T(8,128)(2,1)}, bf16[3584,896]{1,0:T(8,128)(2,1)}) custom-call(s32[1]{0:T(128)} %bitcast.2.device_ref, bf16[112,2048]{1,0:T(8,128)(2,1)} %collective-permute-done.3.refs_0_, bf16[112,2048]{1,0:T(8,128)(2,1)} %collective-permute-done.4.refs_1_, ...), custom_call_target="tpu_custom_call", output_to_operand_aliasing={{0}: (3, {}), {1}: (4, {})} | custom-call | tf_op jit(solution)/shard_map/pallas_call | solution.py:61
  (92 shorter events, 3.2 us)
Async XLA Ops:
  3.6 34.5 %collective-permute-start.5 = (bf16[112,2048]{1,0:T(8,128)(2,1)S(1)}, bf16[112,2048]{1,0:T(8,128)(2,1)}, u32[]{:S(2)}, u32[]{:S(2)}) collective-permute-start(bf16[112,2048]{1,0:T(8,128)(2,1)S(1)} %pad_maximum_fusion.1.refs_0_), channel_id=1, source_target_pairs={{0,8},{8,16},{16,24},{24,0},{1,9},{9,17},{17,25},{25,1},{2,10},{10... | collective-permute-start | bytes 1376264 | tf_op jit(solution)/shard_map/ppermute | solution.py:96
  6.7 31.5 %collective-permute-start.23 = (bf16[112,2048]{1,0:T(8,128)(2,1)S(1)}, bf16[112,2048]{1,0:T(8,128)(2,1)}, u32[]{:S(2)}, u32[]{:S(2)}) collective-permute-start(bf16[112,2048]{1,0:T(8,128)(2,1)S(1)} %pad_maximum_fusion.1.refs_0_), channel_id=1, source_target_pairs={{0,4},{4,0},{1,5},{5,1},{2,6},{6,2},{3,7},{7,3},{8,12},{12,8},{9,1... | collective-permute-start | bytes 1376264 | tf_op jit(solution)/shard_map/ppermute | solution.py:99
  6.8 27.7 %collective-permute-start.8 = (bf16[112,2048]{1,0:T(8,128)(2,1)S(1)}, bf16[112,2048]{1,0:T(8,128)(2,1)}, u32[]{:S(2)}, u32[]{:S(2)}) collective-permute-start(bf16[112,2048]{1,0:T(8,128)(2,1)S(1)} %pad_maximum_fusion.2), channel_id=1, source_target_pairs={{0,1},{1,0},{2,3},{3,2},{4,5},{5,4},{6,7},{7,6},{8,9},{9,8},{10,11... | collective-permute-start | bytes 1376264 | tf_op jit(solution)/shard_map/ppermute | solution.py:93
  8.4 28.0 %collective-permute-start.12 = (bf16[112,2048]{1,0:T(8,128)(2,1)S(1)}, bf16[112,2048]{1,0:T(8,128)(2,1)}, u32[]{:S(2)}, u32[]{:S(2)}) collective-permute-start(bf16[112,2048]{1,0:T(8,128)(2,1)S(1)} %pad_maximum_fusion.3), channel_id=1, source_target_pairs={{0,2},{1,3},{2,0},{3,1},{4,6},{5,7},{6,4},{7,5},{8,10},{9,11},{10,... | collective-permute-start | bytes 1376264 | tf_op jit(solution)/shard_map/ppermute | solution.py:93
  10.8 25.7 %collective-permute-start = (bf16[112,2048]{1,0:T(8,128)(2,1)}, bf16[112,2048]{1,0:T(8,128)(2,1)}, u32[]{:S(2)}, u32[]{:S(2)}) collective-permute-start(bf16[112,2048]{1,0:T(8,128)(2,1)} %pad_maximum_fusion), channel_id=1, source_target_pairs={{0,3},{1,2},{2,1},{3,0},{4,7},{5,6},{6,5},{7,4},{8,11},{9,10},{10,... | collective-permute-start | bytes 1376264 | tf_op jit(solution)/shard_map/ppermute | solution.py:93
  34.5 15.6 %collective-permute-start.9 = (bf16[112,2048]{1,0:T(8,128)(2,1)}, bf16[112,2048]{1,0:T(8,128)(2,1)}, u32[]{:S(2)}, u32[]{:S(2)}) collective-permute-start(bf16[112,2048]{1,0:T(8,128)(2,1)} %collective-permute-done.8.refs_1_), channel_id=1, source_target_pairs={{0,8},{8,16},{16,24},{24,0},{1,9},{9,17},{17,25},{25,1},{2,10},{10... | collective-permute-start | bytes 1376264 | tf_op jit(solution)/shard_map/ppermute | solution.py:96
  36.4 30.9 %collective-permute-start.24 = (bf16[112,2048]{1,0:T(8,128)(2,1)}, bf16[112,2048]{1,0:T(8,128)(2,1)S(1)}, u32[]{:S(2)}, u32[]{:S(2)}) collective-permute-start(bf16[112,2048]{1,0:T(8,128)(2,1)} %collective-permute-done.8.refs_1_), channel_id=1, source_target_pairs={{0,4},{4,0},{1,5},{5,1},{2,6},{6,2},{3,7},{7,3},{8,12},{12,8},{9,1... | collective-permute-start | bytes 1376264 | tf_op jit(solution)/shard_map/ppermute | solution.py:99
  36.5 23.4 %collective-permute-start.13 = (bf16[112,2048]{1,0:T(8,128)(2,1)}, bf16[112,2048]{1,0:T(8,128)(2,1)}, u32[]{:S(2)}, u32[]{:S(2)}) collective-permute-start(bf16[112,2048]{1,0:T(8,128)(2,1)} %collective-permute-done.12.refs_2_), channel_id=1, source_target_pairs={{0,8},{8,16},{16,24},{24,0},{1,9},{9,17},{17,25},{25,1},{2,10},{10... | collective-permute-start | bytes 1376264 | tf_op jit(solution)/shard_map/ppermute | solution.py:96
  38.1 29.3 %collective-permute-start.25 = (bf16[112,2048]{1,0:T(8,128)(2,1)}, bf16[112,2048]{1,0:T(8,128)(2,1)}, u32[]{:S(2)}, u32[]{:S(2)}) collective-permute-start(bf16[112,2048]{1,0:T(8,128)(2,1)} %collective-permute-done.12.refs_2_), channel_id=1, source_target_pairs={{0,4},{4,0},{1,5},{5,1},{2,6},{6,2},{3,7},{7,3},{8,12},{12,8},{9,1... | collective-permute-start | bytes 1376264 | tf_op jit(solution)/shard_map/ppermute | solution.py:99
  38.2 29.0 %collective-permute-start.1 = (bf16[112,2048]{1,0:T(8,128)(2,1)}, bf16[112,2048]{1,0:T(8,128)(2,1)S(1)}, u32[]{:S(2)}, u32[]{:S(2)}) collective-permute-start(bf16[112,2048]{1,0:T(8,128)(2,1)} %collective-permute-done.refs_3_), channel_id=1, source_target_pairs={{0,8},{8,16},{16,24},{24,0},{1,9},{9,17},{17,25},{25,1},{2,10},{10... | collective-permute-start | bytes 1376264 | tf_op jit(solution)/shard_map/ppermute | solution.py:96
  50.0 17.9 %collective-permute-start.26 = (bf16[112,2048]{1,0:T(8,128)(2,1)}, bf16[112,2048]{1,0:T(8,128)(2,1)}, u32[]{:S(2)}, u32[]{:S(2)}) collective-permute-start(bf16[112,2048]{1,0:T(8,128)(2,1)} %collective-permute-done.refs_3_), channel_id=1, source_target_pairs={{0,4},{4,0},{1,5},{5,1},{2,6},{6,2},{3,7},{7,3},{8,12},{12,8},{9,1... | collective-permute-start | bytes 1376264 | tf_op jit(solution)/shard_map/ppermute | solution.py:99
  59.8 9.0 %collective-permute-start.27 = (bf16[112,2048]{1,0:T(8,128)(2,1)}, bf16[112,2048]{1,0:T(8,128)(2,1)S(1)}, u32[]{:S(2)}, u32[]{:S(2)}) collective-permute-start(bf16[112,2048]{1,0:T(8,128)(2,1)} %collective-permute-done.5.refs_4_), channel_id=1, source_target_pairs={{0,4},{4,0},{1,5},{5,1},{2,6},{6,2},{3,7},{7,3},{8,12},{12,8},{9,1... | collective-permute-start | bytes 1376264 | tf_op jit(solution)/shard_map/ppermute | solution.py:99
  67.3 85.7 %copy-start.3 = (bf16[112,2048]{1,0:T(8,128)(2,1)}, bf16[112,2048]{1,0:T(8,128)(2,1)S(1)}, u32[]{:S(2)}) copy-start(bf16[112,2048]{1,0:T(8,128)(2,1)S(1)} %collective-permute-done.1.refs_7_) | copy-start | bytes 1376260
  67.3 15.5 %collective-permute-start.6 = (bf16[112,2048]{1,0:T(8,128)(2,1)}, bf16[112,2048]{1,0:T(8,128)(2,1)}, u32[]{:S(2)}, u32[]{:S(2)}) collective-permute-start(bf16[112,2048]{1,0:T(8,128)(2,1)} %collective-permute-done.5.refs_4_), channel_id=1, source_target_pairs={{0,8},{8,16},{16,24},{24,0},{1,9},{9,17},{17,25},{25,1},{2,10},{10... | collective-permute-start | bytes 1376264 | tf_op jit(solution)/shard_map/ppermute | solution.py:96
  67.3 15.5 %collective-permute-start.28 = (bf16[112,2048]{1,0:T(8,128)(2,1)}, bf16[112,2048]{1,0:T(8,128)(2,1)S(1)}, u32[]{:S(2)}, u32[]{:S(2)}) collective-permute-start(bf16[112,2048]{1,0:T(8,128)(2,1)} %collective-permute-done.9.refs_5_), channel_id=1, source_target_pairs={{0,4},{4,0},{1,5},{5,1},{2,6},{6,2},{3,7},{7,3},{8,12},{12,8},{9,1... | collective-permute-start | bytes 1376264 | tf_op jit(solution)/shard_map/ppermute | solution.py:99
  67.4 15.5 %collective-permute-start.29 = (bf16[112,2048]{1,0:T(8,128)(2,1)}, bf16[112,2048]{1,0:T(8,128)(2,1)S(1)}, u32[]{:S(2)}, u32[]{:S(2)}) collective-permute-start(bf16[112,2048]{1,0:T(8,128)(2,1)} %collective-permute-done.13.refs_6_), channel_id=1, source_target_pairs={{0,4},{4,0},{1,5},{5,1},{2,6},{6,2},{3,7},{7,3},{8,12},{12,8},{9,1... | collective-permute-start | bytes 1376264 | tf_op jit(solution)/shard_map/ppermute | solution.py:99
  67.9 15.1 %collective-permute-start.30 = (bf16[112,2048]{1,0:T(8,128)(2,1)S(1)}, bf16[112,2048]{1,0:T(8,128)(2,1)S(1)}, u32[]{:S(2)}, u32[]{:S(2)}) collective-permute-start(bf16[112,2048]{1,0:T(8,128)(2,1)S(1)} %collective-permute-done.1.refs_7_), channel_id=1, source_target_pairs={{0,4},{4,0},{1,5},{5,1},{2,6},{6,2},{3,7},{7,3},{8,12},{12,8},{9,1... | collective-permute-start | bytes 1376264 | tf_op jit(solution)/shard_map/ppermute | solution.py:99
  68.8 26.2 %collective-permute-start.10 = (bf16[112,2048]{1,0:T(8,128)(2,1)}, bf16[112,2048]{1,0:T(8,128)(2,1)}, u32[]{:S(2)}, u32[]{:S(2)}) collective-permute-start(bf16[112,2048]{1,0:T(8,128)(2,1)} %collective-permute-done.9.refs_5_), channel_id=1, source_target_pairs={{0,8},{8,16},{16,24},{24,0},{1,9},{9,17},{17,25},{25,1},{2,10},{10... | collective-permute-start | bytes 1376264 | tf_op jit(solution)/shard_map/ppermute | solution.py:96
  82.8 19.7 %collective-permute-start.14 = (bf16[112,2048]{1,0:T(8,128)(2,1)}, bf16[112,2048]{1,0:T(8,128)(2,1)}, u32[]{:S(2)}, u32[]{:S(2)}) collective-permute-start(bf16[112,2048]{1,0:T(8,128)(2,1)} %collective-permute-done.13.refs_6_), channel_id=1, source_target_pairs={{0,8},{8,16},{16,24},{24,0},{1,9},{9,17},{17,25},{25,1},{2,10},{10... | collective-permute-start | bytes 1376264 | tf_op jit(solution)/shard_map/ppermute | solution.py:96
  82.8 29.5 %collective-permute-start.2 = (bf16[112,2048]{1,0:T(8,128)(2,1)S(1)}, bf16[112,2048]{1,0:T(8,128)(2,1)}, u32[]{:S(2)}, u32[]{:S(2)}) collective-permute-start(bf16[112,2048]{1,0:T(8,128)(2,1)S(1)} %collective-permute-done.1.refs_7_), channel_id=1, source_target_pairs={{0,8},{8,16},{16,24},{24,0},{1,9},{9,17},{17,25},{25,1},{2,10},{10... | collective-permute-start | bytes 1376264 | tf_op jit(solution)/shard_map/ppermute | solution.py:96
  82.9 29.4 %collective-permute-start.19 = (bf16[112,2048]{1,0:T(8,128)(2,1)}, bf16[112,2048]{1,0:T(8,128)(2,1)}, u32[]{:S(2)}, u32[]{:S(2)}) collective-permute-start(bf16[112,2048]{1,0:T(8,128)(2,1)} %collective-permute-done.6.refs_0_), channel_id=1, source_target_pairs={{0,4},{4,0},{1,5},{5,1},{2,6},{6,2},{3,7},{7,3},{8,12},{12,8},{9,1... | collective-permute-start | bytes 1376264 | tf_op jit(solution)/shard_map/ppermute | solution.py:99
  83.0 39.1 %collective-permute-start.7 = (bf16[112,2048]{1,0:T(8,128)(2,1)}, bf16[112,2048]{1,0:T(8,128)(2,1)}, u32[]{:S(2)}, u32[]{:S(2)}) collective-permute-start(bf16[112,2048]{1,0:T(8,128)(2,1)} %collective-permute-done.6.refs_0_), channel_id=1, source_target_pairs={{0,8},{8,16},{16,24},{24,0},{1,9},{9,17},{17,25},{25,1},{2,10},{10... | collective-permute-start | bytes 1376264 | tf_op jit(solution)/shard_map/ppermute | solution.py:96
  95.0 43.7 %collective-permute-start.20 = (bf16[112,2048]{1,0:T(8,128)(2,1)}, bf16[112,2048]{1,0:T(8,128)(2,1)}, u32[]{:S(2)}, u32[]{:S(2)}) collective-permute-start(bf16[112,2048]{1,0:T(8,128)(2,1)} %collective-permute-done.10.refs_1_), channel_id=1, source_target_pairs={{0,4},{4,0},{1,5},{5,1},{2,6},{6,2},{3,7},{7,3},{8,12},{12,8},{9,1... | collective-permute-start | bytes 1376264 | tf_op jit(solution)/shard_map/ppermute | solution.py:99
  102.5 36.8 %collective-permute-start.11 = (bf16[112,2048]{1,0:T(8,128)(2,1)}, bf16[112,2048]{1,0:T(8,128)(2,1)}, u32[]{:S(2)}, u32[]{:S(2)}) collective-permute-start(bf16[112,2048]{1,0:T(8,128)(2,1)} %collective-permute-done.10.refs_1_), channel_id=1, source_target_pairs={{0,8},{8,16},{16,24},{24,0},{1,9},{9,17},{17,25},{25,1},{2,10},{10... | collective-permute-start | bytes 1376264 | tf_op jit(solution)/shard_map/ppermute | solution.py:96
  112.3 26.5 %collective-permute-start.21 = (bf16[112,2048]{1,0:T(8,128)(2,1)}, bf16[112,2048]{1,0:T(8,128)(2,1)}, u32[]{:S(2)}, u32[]{:S(2)}) collective-permute-start(bf16[112,2048]{1,0:T(8,128)(2,1)} %collective-permute-done.14.refs_2_), channel_id=1, source_target_pairs={{0,4},{4,0},{1,5},{5,1},{2,6},{6,2},{3,7},{7,3},{8,12},{12,8},{9,1... | collective-permute-start | bytes 1376264 | tf_op jit(solution)/shard_map/ppermute | solution.py:99
  112.3 29.5 %collective-permute-start.15 = (bf16[112,2048]{1,0:T(8,128)(2,1)}, bf16[112,2048]{1,0:T(8,128)(2,1)}, u32[]{:S(2)}, u32[]{:S(2)}) collective-permute-start(bf16[112,2048]{1,0:T(8,128)(2,1)} %collective-permute-done.14.refs_2_), channel_id=1, source_target_pairs={{0,8},{8,16},{16,24},{24,0},{1,9},{9,17},{17,25},{25,1},{2,10},{10... | collective-permute-start | bytes 1376264 | tf_op jit(solution)/shard_map/ppermute | solution.py:96
  122.1 26.3 %collective-permute-start.3 = (bf16[112,2048]{1,0:T(8,128)(2,1)}, bf16[112,2048]{1,0:T(8,128)(2,1)}, u32[]{:S(2)}, u32[]{:S(2)}) collective-permute-start(bf16[112,2048]{1,0:T(8,128)(2,1)} %collective-permute-done.2.refs_3_), channel_id=1, source_target_pairs={{0,8},{8,16},{16,24},{24,0},{1,9},{9,17},{17,25},{25,1},{2,10},{10... | collective-permute-start | bytes 1376264 | tf_op jit(solution)/shard_map/ppermute | solution.py:96
  138.7 238.1 %collective-permute-start.22 = (bf16[112,2048]{1,0:T(8,128)(2,1)}, bf16[112,2048]{1,0:T(8,128)(2,1)}, u32[]{:S(2)}, u32[]{:S(2)}) collective-permute-start(bf16[112,2048]{1,0:T(8,128)(2,1)} %collective-permute-done.2.refs_3_), channel_id=1, source_target_pairs={{0,4},{4,0},{1,5},{5,1},{2,6},{6,2},{3,7},{7,3},{8,12},{12,8},{9,1... | collective-permute-start | bytes 1376264 | tf_op jit(solution)/shard_map/ppermute | solution.py:99
  138.8 350.4 %collective-permute-start.16 = (bf16[112,2048]{1,0:T(8,128)(2,1)}, bf16[112,2048]{1,0:T(8,128)(2,1)}, u32[]{:S(2)}, u32[]{:S(2)}) collective-permute-start(bf16[112,2048]{1,0:T(8,128)(2,1)} %collective-permute-done.7.refs_0_), channel_id=1, source_target_pairs={{0,4},{4,0},{1,5},{5,1},{2,6},{6,2},{3,7},{7,3},{8,12},{12,8},{9,1... | collective-permute-start | bytes 1376264 | tf_op jit(solution)/shard_map/ppermute | solution.py:99
  139.3 349.9 %collective-permute-start.17 = (bf16[112,2048]{1,0:T(8,128)(2,1)}, bf16[112,2048]{1,0:T(8,128)(2,1)}, u32[]{:S(2)}, u32[]{:S(2)}) collective-permute-start(bf16[112,2048]{1,0:T(8,128)(2,1)} %collective-permute-done.11.refs_1_), channel_id=1, source_target_pairs={{0,4},{4,0},{1,5},{5,1},{2,6},{6,2},{3,7},{7,3},{8,12},{12,8},{9,1... | collective-permute-start | bytes 1376264 | tf_op jit(solution)/shard_map/ppermute | solution.py:99
  141.8 347.5 %collective-permute-start.18 = (bf16[112,2048]{1,0:T(8,128)(2,1)}, bf16[112,2048]{1,0:T(8,128)(2,1)}, u32[]{:S(2)}, u32[]{:S(2)}) collective-permute-start(bf16[112,2048]{1,0:T(8,128)(2,1)} %collective-permute-done.15.refs_2_), channel_id=1, source_target_pairs={{0,4},{4,0},{1,5},{5,1},{2,6},{6,2},{3,7},{7,3},{8,12},{12,8},{9,1... | collective-permute-start | bytes 1376264 | tf_op jit(solution)/shard_map/ppermute | solution.py:99
  148.5 425.4 %collective-permute-start.4 = (bf16[112,2048]{1,0:T(8,128)(2,1)}, bf16[112,2048]{1,0:T(8,128)(2,1)}, u32[]{:S(2)}, u32[]{:S(2)}) collective-permute-start(bf16[112,2048]{1,0:T(8,128)(2,1)} %collective-permute-done.3.refs_0_), channel_id=1, source_target_pairs={{0,4},{4,0},{1,5},{5,1},{2,6},{6,2},{3,7},{7,3},{8,12},{12,8},{9,1... | collective-permute-start | bytes 1376264 | tf_op jit(solution)/shard_map/ppermute | solution.py:99
  (9 other events, 216.2 us)

commit v2 on v1

--- a/solution.py
+++ b/solution.py
@@ -62,10 +62,14 @@
         kernel,
         out_shape=[jax.ShapeDtypeStruct((total_rows, width), dtype) for width in widths],
         in_specs=[pl.BlockSpec(memory_space=pltpu.SMEM)]
-        + [pl.BlockSpec(memory_space=pl.ANY)] * (count + aliased),
+        + [pl.BlockSpec(memory_space=pltpu.VMEM)] * count
+        + [pl.BlockSpec(memory_space=pl.ANY)] * aliased,
         out_specs=[pl.BlockSpec(memory_space=pl.ANY)] * len(widths),
         scratch_shapes=[pltpu.SemaphoreType.DMA((count, len(widths)))],
         input_output_aliases={1 + count + at: at for at in range(aliased)},
+        compiler_params=pltpu.CompilerParams(
+            vmem_limit_bytes=count * pieces[0].size * dtype.itemsize + (2 << 20)
+        ),
     )(device, *pieces, *(() if outs is None else outs))
 
 

time: 603 us -> 171 us (0.28)
  Pallas kernels: 450 us -> 14.8 us
  waiting for transfers between devices: 77.1 us -> 63.5 us
  other arithmetic: 1.9 us -> 8.98 us
  local copies, waits for them, and re-layouts: 3.36 us -> 10.4 us
    pallas_call x4, Pallas kernels: 450 us -> 14.8 us  [place_pieces(): pl.pallas_call(kernel, out_shape=[jax.ShapeDtypeStruct((total_rows, width...]
    ppermute x12, waiting for transfers between devices: 77 us -> 63.4 us  [reshard_by_permutes(): mine[s, j] = lax.ppermute(mine[s - 1, j], 'outer', ring)]
  transfers between devices with their start and end apart: 31 -> 31, of which waited for: 9 -> 8; matrix products, arithmetic and copies ran while one was open for 2% -> 15% of each run, Pallas kernels for 70% -> 7%
where the time goes in v2:
time: 171 us; the launch traced here: 170 us
  waiting for transfers between devices  63.5 us (37%)
  blocking collectives  44.7 us (26%)
  Pallas kernels  14.8 us (9%)
  starting transfers between devices  14 us (8%)
  matrix products  12.6 us (7%)
  local copies, waits for them, and re-layouts  10.4 us (6%)
  other arithmetic  8.98 us (5%)
    ppermute x12, waiting for transfers between devices, reshard_by_permutes(): mine[s, j] = lax.ppermute(mine[s - 1, j], 'outer', ring)  63.4 us
    all_gather x1, blocking collectives, decode(): joined_rows = lax.all_gather(local_joined, 'tp', axis=1, tiled=True)  18.8 us
    psum x1, blocking collectives, decode(): numerator, denominator = lax.psum((numer_part, denom_part), 'tp')  16.9 us
    pallas_call x4, Pallas kernels, place_pieces(): pl.pallas_call(kernel, out_shape=[jax.ShapeDtypeStruct((total_rows, width...  14.8 us
    pmax x1, blocking collectives, decode(): top_score = lax.pmax(local_top, 'tp')  9.1 us
    ppermute x12, starting transfers between devices, reshard_by_permutes(): mine[s, j] = lax.ppermute(mine[s - 1, j], 'outer', ring)  8.63 us
    dot_general x1, matrix products, decode(): jnp.dot(hidden_state, old_qkv, preferred_element_type=jnp.float32)  4.51 us
    dot_general x1, matrix products, decode(): jnp.dot(attended, old_out, preferred_element_type=jnp.float32)  4.5 us
  transfers between devices with their start and end apart: 31, of which 8 were waited for; matrix products, arithmetic and copies ran while one was open for 15% of the time, Pallas kernels for 7%

profile of v2, /device:TPU:0, one launch (start us, length us, event | category | flops | bytes accessed | tf_op | source)
XLA Modules:
  0.0 169.9 jit_solution(11446548982464025770)
XLA Ops:
  0.7 1.6 constant_dynamic-slice_fusion.1
  2.3 1.3 constant_dynamic-slice_fusion
  3.6 3.1 %collective-permute-start.5 = (bf16[112,2048]{1,0:T(8,128)(2,1)S(1)}, bf16[112,2048]{1,0:T(8,128)(2,1)S(1)}, u32[]{:S(2)}, u32[]{:S(2)}) collective-permute-start(bf16[112,2048]{1,0:T(8,128)(2,1)S(1)} %pad_maximum_fusion.1.refs_0_), channel_id=1, source_target_pairs={{0,8},{8,16},{16,24},{24,0},{1,9},{9,17},{17,25},{25,1},{2,10},{10... | collective-permute-start | bytes 1376264 | tf_op jit(solution)/shard_map/ppermute | solution.py:100
  6.8 1.6 collective-permute-start.8
  9.1 1.5 collective-permute-start.12
  12.0 4.5 %convolution_convert_fusion = bf16[4,1152]{1,0:T(4,128)(2,1)S(1)} fusion(bf16[4,3584]{1,0:T(4,128)(2,1)S(1)} %copy-done.10, bf16[3584,1152]{1,0:T(8,128)(2,1)} %param.10), kind=kOutput, calls=%fused_computation | convolution fusion | flops 33034752 | bytes 8295424 | tf_op jit(solution)/shard_map/dot_general | solution.py:148
  16.5 18.8 %all_gather.3 = bf16[4,4608]{1,0:T(4,128)(2,1)S(1)} all-gather(bf16[4,1152]{1,0:T(4,128)(2,1)S(1)} %convolution_convert_fusion), channel_id=1, replica_groups=mesh['outer'=4,'core'=2,'tp'=4] {'tp'}, dimensions={1}, use_global_device_ids=true | all-gather | bytes 46080 | tf_op jit(solution)/shard_map/all_gather | solution.py:151
  35.9 1.6 collective-permute-start.9
  37.6 0.9 reshape.155
  38.5 1.3 slice_convert_fusion.1
  40.5 1.6 collective-permute-start.13
  42.7 8.8 %collective-permute-done.9.refs_5_ = bf16[112,2048]{1,0:T(8,128)(2,1)} collective-permute-done((bf16[112,2048]{1,0:T(8,128)(2,1)}, bf16[112,2048]{1,0:T(8,128)(2,1)}, u32[]{:S(2)}, u32[]{:S(2)}) %collective-permute-start.9) | collective-permute-done | bytes 458784 | tf_op jit(solution)/shard_map/ppermute | solution.py:100
  53.4 7.9 %collective-permute-done.13.refs_6_ = bf16[112,2048]{1,0:T(8,128)(2,1)} collective-permute-done((bf16[112,2048]{1,0:T(8,128)(2,1)}, bf16[112,2048]{1,0:T(8,128)(2,1)}, u32[]{:S(2)}, u32[]{:S(2)}) %collective-permute-start.13) | collective-permute-done | bytes 458784 | tf_op jit(solution)/shard_map/ppermute | solution.py:100
  61.3 7.4 %collective-permute-done.1.refs_7_ = bf16[112,2048]{1,0:T(8,128)(2,1)} collective-permute-done((bf16[112,2048]{1,0:T(8,128)(2,1)}, bf16[112,2048]{1,0:T(8,128)(2,1)}, u32[]{:S(2)}, u32[]{:S(2)}) %collective-permute-start.1) | collective-permute-done | bytes 458784 | tf_op jit(solution)/shard_map/ppermute | solution.py:100
  70.0 1.4 fusion.14
  72.2 1.3 collective-permute-start.10
  73.5 10.2 %collective-permute-done.6.refs_0_ = bf16[112,2048]{1,0:T(8,128)(2,1)} collective-permute-done((bf16[112,2048]{1,0:T(8,128)(2,1)S(1)}, bf16[112,2048]{1,0:T(8,128)(2,1)}, u32[]{:S(2)}, u32[]{:S(2)}) %collective-permute-start.6) | collective-permute-done | bytes 458784 | tf_op jit(solution)/shard_map/ppermute | solution.py:100
  86.7 9.1 %pmax.7 = f32[4,4,7]{2,1,0:T(4,128)S(1)} all-reduce(f32[4,4,7]{2,1,0:T(4,128)S(1)} %multiply_maximum_fusion), channel_id=1, replica_groups=mesh['outer'=4,'core'=2,'tp'=4] {'tp'}, use_global_device_ids=true, to_apply=%region_2.3 | all-reduce | flops 112 | bytes 896 | tf_op jit(solution)/shard_map/pmax | solution.py:180
  95.8 2.1 %fusion = f32[4,4,7,128]{3,2,1,0:T(8,128)S(1)} fusion(f32[4,4,7,512]{3,2,1,0:T(8,128)} %get-tuple-element.38, f32[4,4,7]{2,1,0:T(4,128)S(1)} %pmax.7, pred[4,512]{1,0:T(4,128)(4,1)} %copy-done.12, bf16[4,512,512]{2,1,0:T(8,128)(2,1)} %param.13), kind=kOutput, calls=%fused_computation.1 | convolution fusion | flops 14852096 | bytes 2386368 | tf_op jit(solution)/shard_map/skgt,stkd->skgd/dot_general | solution.py:184
  98.0 5.4 %collective-permute-done.14.refs_2_ = bf16[112,2048]{1,0:T(8,128)(2,1)} collective-permute-done((bf16[112,2048]{1,0:T(8,128)(2,1)}, bf16[112,2048]{1,0:T(8,128)(2,1)}, u32[]{:S(2)}, u32[]{:S(2)}) %collective-permute-start.14) | collective-permute-done | bytes 458784 | tf_op jit(solution)/shard_map/ppermute | solution.py:100
  103.4 9.8 %collective-permute-done.2.refs_3_ = bf16[112,2048]{1,0:T(8,128)(2,1)} collective-permute-done((bf16[112,2048]{1,0:T(8,128)(2,1)}, bf16[112,2048]{1,0:T(8,128)(2,1)}, u32[]{:S(2)}, u32[]{:S(2)}) %collective-permute-start.2) | collective-permute-done | bytes 458784 | tf_op jit(solution)/shard_map/ppermute | solution.py:100
  113.2 9.8 %collective-permute-done.7.refs_0_ = bf16[112,2048]{1,0:T(8,128)(2,1)} collective-permute-done((bf16[112,2048]{1,0:T(8,128)(2,1)}, bf16[112,2048]{1,0:T(8,128)(2,1)}, u32[]{:S(2)}, u32[]{:S(2)}) %collective-permute-start.7) | collective-permute-done | bytes 458784 | tf_op jit(solution)/shard_map/ppermute | solution.py:100
  124.3 1.3 reshape.158
  125.6 1.2 convert_reduce_fusion
  126.7 16.9 %all-reduce = (f32[4,4,7,128]{3,2,1,0:T(8,128)}, f32[4,4,7]{2,1,0:T(4,128)S(1)}) all-reduce(f32[4,4,7,128]{3,2,1,0:T(8,128)S(1)} %fusion, f32[4,4,7]{2,1,0:T(4,128)S(1)} %convert_reduce_fusion), channel_id=1, replica_groups=mesh['outer'=4,'core'=2,'tp'=4] {'tp'}, use_global_device_ids=true, to_apply=%region_3.4 | all-reduce | flops 14448 | bytes 115584 | tf_op jit(solution)/shard_map/psum | solution.py:188
  145.3 4.2 %collective-permute-done.3.refs_0_ = bf16[112,2048]{1,0:T(8,128)(2,1)} collective-permute-done((bf16[112,2048]{1,0:T(8,128)(2,1)}, bf16[112,2048]{1,0:T(8,128)(2,1)}, u32[]{:S(2)}, u32[]{:S(2)}) %collective-permute-start.3) | collective-permute-done | bytes 458784 | tf_op jit(solution)/shard_map/ppermute | solution.py:100
  149.5 1.0 divide_convert_fusion
  150.5 4.5 %convolution_convert_fusion.1 = bf16[4,896]{1,0:T(4,128)(2,1)} fusion(bf16[4,3584]{1,0:T(4,128)(2,1)S(1)} %convert_element_type.68, bf16[3584,896]{1,0:T(8,128)(2,1)} %param.11), kind=kOutput, calls=%fused_computation.9 | convolution fusion | flops 25693696 | bytes 6458368 | tf_op jit(solution)/shard_map/dot_general | solution.py:195
  155.1 5.4 %shard_map.103 = (bf16[3584,1152]{1,0:T(8,128)(2,1)}, bf16[3584,896]{1,0:T(8,128)(2,1)}) custom-call(s32[1]{0:T(128)} %bitcast.2.device_ref, bf16[112,2048]{1,0:T(8,128)(2,1)S(1)} %pad_maximum_fusion.1.refs_0_, bf16[112,2048]{1,0:T(8,128)(2,1)} %collective-permute-done.8.refs_1_, bf16[112,2048]{1,0:T(8,128)(2,1)} %collective-permute-done.12.refs_2_, ...), custom_call_target="tpu_custom_call" | custom-call | tf_op jit(solution)/shard_map/pallas_call | solution.py:61
  160.5 4.0 %shard_map.104 = (bf16[3584,1152]{1,0:T(8,128)(2,1)}, bf16[3584,896]{1,0:T(8,128)(2,1)}) custom-call(s32[1]{0:T(128)} %bitcast.2.device_ref, bf16[112,2048]{1,0:T(8,128)(2,1)} %collective-permute-done.6.refs_0_, bf16[112,2048]{1,0:T(8,128)(2,1)} %collective-permute-done.10.refs_1_, ...), custom_call_target="tpu_custom_call", output_to_operand_aliasing={{0}: (9, {}), {1}: (10, {})} | custom-call | tf_op jit(solution)/shard_map/pallas_call | solution.py:61
  164.5 3.3 %shard_map.105 = (bf16[3584,1152]{1,0:T(8,128)(2,1)}, bf16[3584,896]{1,0:T(8,128)(2,1)}) custom-call(s32[1]{0:T(128)} %bitcast.2.device_ref, bf16[112,2048]{1,0:T(8,128)(2,1)} %collective-permute-done.7.refs_0_, bf16[112,2048]{1,0:T(8,128)(2,1)} %collective-permute-done.11.refs_1_, ...), custom_call_target="tpu_custom_call", output_to_operand_aliasing={{0}: (7, {}), {1}: (8, {})} | custom-call | tf_op jit(solution)/shard_map/pallas_call | solution.py:61
  167.8 2.1 %shard_map.106 = (bf16[3584,1152]{1,0:T(8,128)(2,1)}, bf16[3584,896]{1,0:T(8,128)(2,1)}) custom-call(s32[1]{0:T(128)} %bitcast.2.device_ref, bf16[112,2048]{1,0:T(8,128)(2,1)} %collective-permute-done.3.refs_0_, bf16[112,2048]{1,0:T(8,128)(2,1)} %collective-permute-done.4.refs_1_, ...), custom_call_target="tpu_custom_call", output_to_operand_aliasing={{0}: (3, {}), {1}: (4, {})} | custom-call | tf_op jit(solution)/shard_map/pallas_call | solution.py:61
  (100 shorter events, 14.2 us)
Async XLA Ops:
  0.6 69.4 %copy-start = (bf16[4,512,512]{2,1,0:T(8,128)(2,1)S(1)}, bf16[4,512,512]{2,1,0:T(8,128)(2,1)}, u32[]{:S(2)}) copy-start(bf16[4,512,512]{2,1,0:T(8,128)(2,1)} %param.12) | copy-start | bytes 6291460
  3.6 38.6 %collective-permute-start.5 = (bf16[112,2048]{1,0:T(8,128)(2,1)S(1)}, bf16[112,2048]{1,0:T(8,128)(2,1)S(1)}, u32[]{:S(2)}, u32[]{:S(2)}) collective-permute-start(bf16[112,2048]{1,0:T(8,128)(2,1)S(1)} %pad_maximum_fusion.1.refs_0_), channel_id=1, source_target_pairs={{0,8},{8,16},{16,24},{24,0},{1,9},{9,17},{17,25},{25,1},{2,10},{10... | collective-permute-start | bytes 1376264 | tf_op jit(solution)/shard_map/ppermute | solution.py:100
  6.7 35.6 %collective-permute-start.23 = (bf16[112,2048]{1,0:T(8,128)(2,1)S(1)}, bf16[112,2048]{1,0:T(8,128)(2,1)S(1)}, u32[]{:S(2)}, u32[]{:S(2)}) collective-permute-start(bf16[112,2048]{1,0:T(8,128)(2,1)S(1)} %pad_maximum_fusion.1.refs_0_), channel_id=1, source_target_pairs={{0,4},{4,0},{1,5},{5,1},{2,6},{6,2},{3,7},{7,3},{8,12},{12,8},{9,1... | collective-permute-start | bytes 1376264 | tf_op jit(solution)/shard_map/ppermute | solution.py:103
  6.8 29.1 %collective-permute-start.8 = (bf16[112,2048]{1,0:T(8,128)(2,1)S(1)}, bf16[112,2048]{1,0:T(8,128)(2,1)}, u32[]{:S(2)}, u32[]{:S(2)}) collective-permute-start(bf16[112,2048]{1,0:T(8,128)(2,1)S(1)} %pad_maximum_fusion.2), channel_id=1, source_target_pairs={{0,1},{1,0},{2,3},{3,2},{4,5},{5,4},{6,7},{7,6},{8,9},{9,8},{10,11... | collective-permute-start | bytes 1376264 | tf_op jit(solution)/shard_map/ppermute | solution.py:97
  9.1 31.4 %collective-permute-start.12 = (bf16[112,2048]{1,0:T(8,128)(2,1)}, bf16[112,2048]{1,0:T(8,128)(2,1)}, u32[]{:S(2)}, u32[]{:S(2)}) collective-permute-start(bf16[112,2048]{1,0:T(8,128)(2,1)} %pad_maximum_fusion.3), channel_id=1, source_target_pairs={{0,2},{1,3},{2,0},{3,1},{4,6},{5,7},{6,4},{7,5},{8,10},{9,11},{10,... | collective-permute-start | bytes 1376264 | tf_op jit(solution)/shard_map/ppermute | solution.py:97
  11.5 29.1 %collective-permute-start = (bf16[112,2048]{1,0:T(8,128)(2,1)}, bf16[112,2048]{1,0:T(8,128)(2,1)}, u32[]{:S(2)}, u32[]{:S(2)}) collective-permute-start(bf16[112,2048]{1,0:T(8,128)(2,1)} %pad_maximum_fusion), channel_id=1, source_target_pairs={{0,3},{1,2},{2,1},{3,0},{4,7},{5,6},{6,5},{7,4},{8,11},{9,10},{10,... | collective-permute-start | bytes 1376264 | tf_op jit(solution)/shard_map/ppermute | solution.py:97
  35.9 15.6 %collective-permute-start.9 = (bf16[112,2048]{1,0:T(8,128)(2,1)}, bf16[112,2048]{1,0:T(8,128)(2,1)}, u32[]{:S(2)}, u32[]{:S(2)}) collective-permute-start(bf16[112,2048]{1,0:T(8,128)(2,1)} %collective-permute-done.8.refs_1_), channel_id=1, source_target_pairs={{0,8},{8,16},{16,24},{24,0},{1,9},{9,17},{17,25},{25,1},{2,10},{10... | collective-permute-start | bytes 1376264 | tf_op jit(solution)/shard_map/ppermute | solution.py:100
  40.5 28.2 %collective-permute-start.24 = (bf16[112,2048]{1,0:T(8,128)(2,1)}, bf16[112,2048]{1,0:T(8,128)(2,1)}, u32[]{:S(2)}, u32[]{:S(2)}) collective-permute-start(bf16[112,2048]{1,0:T(8,128)(2,1)} %collective-permute-done.8.refs_1_), channel_id=1, source_target_pairs={{0,4},{4,0},{1,5},{5,1},{2,6},{6,2},{3,7},{7,3},{8,12},{12,8},{9,1... | collective-permute-start | bytes 1376264 | tf_op jit(solution)/shard_map/ppermute | solution.py:103
  40.5 20.8 %collective-permute-start.13 = (bf16[112,2048]{1,0:T(8,128)(2,1)}, bf16[112,2048]{1,0:T(8,128)(2,1)}, u32[]{:S(2)}, u32[]{:S(2)}) collective-permute-start(bf16[112,2048]{1,0:T(8,128)(2,1)} %collective-permute-done.12.refs_2_), channel_id=1, source_target_pairs={{0,8},{8,16},{16,24},{24,0},{1,9},{9,17},{17,25},{25,1},{2,10},{10... | collective-permute-start | bytes 1376264 | tf_op jit(solution)/shard_map/ppermute | solution.py:100
  42.2 26.5 %collective-permute-start.25 = (bf16[112,2048]{1,0:T(8,128)(2,1)}, bf16[112,2048]{1,0:T(8,128)(2,1)}, u32[]{:S(2)}, u32[]{:S(2)}) collective-permute-start(bf16[112,2048]{1,0:T(8,128)(2,1)} %collective-permute-done.12.refs_2_), channel_id=1, source_target_pairs={{0,4},{4,0},{1,5},{5,1},{2,6},{6,2},{3,7},{7,3},{8,12},{12,8},{9,1... | collective-permute-start | bytes 1376264 | tf_op jit(solution)/shard_map/ppermute | solution.py:103
  42.4 26.3 %collective-permute-start.1 = (bf16[112,2048]{1,0:T(8,128)(2,1)}, bf16[112,2048]{1,0:T(8,128)(2,1)}, u32[]{:S(2)}, u32[]{:S(2)}) collective-permute-start(bf16[112,2048]{1,0:T(8,128)(2,1)} %collective-permute-done.refs_3_), channel_id=1, source_target_pairs={{0,8},{8,16},{16,24},{24,0},{1,9},{9,17},{17,25},{25,1},{2,10},{10... | collective-permute-start | bytes 1376264 | tf_op jit(solution)/shard_map/ppermute | solution.py:100
  51.5 17.7 %collective-permute-start.26 = (bf16[112,2048]{1,0:T(8,128)(2,1)}, bf16[112,2048]{1,0:T(8,128)(2,1)}, u32[]{:S(2)}, u32[]{:S(2)}) collective-permute-start(bf16[112,2048]{1,0:T(8,128)(2,1)} %collective-permute-done.refs_3_), channel_id=1, source_target_pairs={{0,4},{4,0},{1,5},{5,1},{2,6},{6,2},{3,7},{7,3},{8,12},{12,8},{9,1... | collective-permute-start | bytes 1376264 | tf_op jit(solution)/shard_map/ppermute | solution.py:103
  61.3 10.1 %collective-permute-start.27 = (bf16[112,2048]{1,0:T(8,128)(2,1)S(1)}, bf16[112,2048]{1,0:T(8,128)(2,1)S(1)}, u32[]{:S(2)}, u32[]{:S(2)}) collective-permute-start(bf16[112,2048]{1,0:T(8,128)(2,1)S(1)} %collective-permute-done.5.refs_4_), channel_id=1, source_target_pairs={{0,4},{4,0},{1,5},{5,1},{2,6},{6,2},{3,7},{7,3},{8,12},{12,8},{9,1... | collective-permute-start | bytes 1376264 | tf_op jit(solution)/shard_map/ppermute | solution.py:103
  68.7 15.0 %collective-permute-start.6 = (bf16[112,2048]{1,0:T(8,128)(2,1)S(1)}, bf16[112,2048]{1,0:T(8,128)(2,1)}, u32[]{:S(2)}, u32[]{:S(2)}) collective-permute-start(bf16[112,2048]{1,0:T(8,128)(2,1)S(1)} %collective-permute-done.5.refs_4_), channel_id=1, source_target_pairs={{0,8},{8,16},{16,24},{24,0},{1,9},{9,17},{17,25},{25,1},{2,10},{10... | collective-permute-start | bytes 1376264 | tf_op jit(solution)/shard_map/ppermute | solution.py:100
  68.7 15.0 %collective-permute-start.28 = (bf16[112,2048]{1,0:T(8,128)(2,1)}, bf16[112,2048]{1,0:T(8,128)(2,1)S(1)}, u32[]{:S(2)}, u32[]{:S(2)}) collective-permute-start(bf16[112,2048]{1,0:T(8,128)(2,1)} %collective-permute-done.9.refs_5_), channel_id=1, source_target_pairs={{0,4},{4,0},{1,5},{5,1},{2,6},{6,2},{3,7},{7,3},{8,12},{12,8},{9,1... | collective-permute-start | bytes 1376264 | tf_op jit(solution)/shard_map/ppermute | solution.py:103
  68.7 15.8 %collective-permute-start.29 = (bf16[112,2048]{1,0:T(8,128)(2,1)}, bf16[112,2048]{1,0:T(8,128)(2,1)S(1)}, u32[]{:S(2)}, u32[]{:S(2)}) collective-permute-start(bf16[112,2048]{1,0:T(8,128)(2,1)} %collective-permute-done.13.refs_6_), channel_id=1, source_target_pairs={{0,4},{4,0},{1,5},{5,1},{2,6},{6,2},{3,7},{7,3},{8,12},{12,8},{9,1... | collective-permute-start | bytes 1376264 | tf_op jit(solution)/shard_map/ppermute | solution.py:103
  69.2 16.1 %collective-permute-start.30 = (bf16[112,2048]{1,0:T(8,128)(2,1)}, bf16[112,2048]{1,0:T(8,128)(2,1)S(1)}, u32[]{:S(2)}, u32[]{:S(2)}) collective-permute-start(bf16[112,2048]{1,0:T(8,128)(2,1)} %collective-permute-done.1.refs_7_), channel_id=1, source_target_pairs={{0,4},{4,0},{1,5},{5,1},{2,6},{6,2},{3,7},{7,3},{8,12},{12,8},{9,1... | collective-permute-start | bytes 1376264 | tf_op jit(solution)/shard_map/ppermute | solution.py:103
  72.2 25.7 %collective-permute-start.10 = (bf16[112,2048]{1,0:T(8,128)(2,1)}, bf16[112,2048]{1,0:T(8,128)(2,1)}, u32[]{:S(2)}, u32[]{:S(2)}) collective-permute-start(bf16[112,2048]{1,0:T(8,128)(2,1)} %collective-permute-done.9.refs_5_), channel_id=1, source_target_pairs={{0,8},{8,16},{16,24},{24,0},{1,9},{9,17},{17,25},{25,1},{2,10},{10... | collective-permute-start | bytes 1376264 | tf_op jit(solution)/shard_map/ppermute | solution.py:100
  83.7 19.7 %collective-permute-start.14 = (bf16[112,2048]{1,0:T(8,128)(2,1)}, bf16[112,2048]{1,0:T(8,128)(2,1)}, u32[]{:S(2)}, u32[]{:S(2)}) collective-permute-start(bf16[112,2048]{1,0:T(8,128)(2,1)} %collective-permute-done.13.refs_6_), channel_id=1, source_target_pairs={{0,8},{8,16},{16,24},{24,0},{1,9},{9,17},{17,25},{25,1},{2,10},{10... | collective-permute-start | bytes 1376264 | tf_op jit(solution)/shard_map/ppermute | solution.py:100
  84.5 28.7 %collective-permute-start.2 = (bf16[112,2048]{1,0:T(8,128)(2,1)}, bf16[112,2048]{1,0:T(8,128)(2,1)}, u32[]{:S(2)}, u32[]{:S(2)}) collective-permute-start(bf16[112,2048]{1,0:T(8,128)(2,1)} %collective-permute-done.1.refs_7_), channel_id=1, source_target_pairs={{0,8},{8,16},{16,24},{24,0},{1,9},{9,17},{17,25},{25,1},{2,10},{10... | collective-permute-start | bytes 1376264 | tf_op jit(solution)/shard_map/ppermute | solution.py:100
  85.3 27.9 %collective-permute-start.19 = (bf16[112,2048]{1,0:T(8,128)(2,1)}, bf16[112,2048]{1,0:T(8,128)(2,1)}, u32[]{:S(2)}, u32[]{:S(2)}) collective-permute-start(bf16[112,2048]{1,0:T(8,128)(2,1)} %collective-permute-done.6.refs_0_), channel_id=1, source_target_pairs={{0,4},{4,0},{1,5},{5,1},{2,6},{6,2},{3,7},{7,3},{8,12},{12,8},{9,1... | collective-permute-start | bytes 1376264 | tf_op jit(solution)/shard_map/ppermute | solution.py:103
  86.1 37.0 %collective-permute-start.7 = (bf16[112,2048]{1,0:T(8,128)(2,1)}, bf16[112,2048]{1,0:T(8,128)(2,1)}, u32[]{:S(2)}, u32[]{:S(2)}) collective-permute-start(bf16[112,2048]{1,0:T(8,128)(2,1)} %collective-permute-done.6.refs_0_), channel_id=1, source_target_pairs={{0,8},{8,16},{16,24},{24,0},{1,9},{9,17},{17,25},{25,1},{2,10},{10... | collective-permute-start | bytes 1376264 | tf_op jit(solution)/shard_map/ppermute | solution.py:100
  97.9 46.4 %collective-permute-start.20 = (bf16[112,2048]{1,0:T(8,128)(2,1)}, bf16[112,2048]{1,0:T(8,128)(2,1)}, u32[]{:S(2)}, u32[]{:S(2)}) collective-permute-start(bf16[112,2048]{1,0:T(8,128)(2,1)} %collective-permute-done.10.refs_1_), channel_id=1, source_target_pairs={{0,4},{4,0},{1,5},{5,1},{2,6},{6,2},{3,7},{7,3},{8,12},{12,8},{9,1... | collective-permute-start | bytes 1376264 | tf_op jit(solution)/shard_map/ppermute | solution.py:103
  103.4 41.4 %collective-permute-start.11 = (bf16[112,2048]{1,0:T(8,128)(2,1)}, bf16[112,2048]{1,0:T(8,128)(2,1)}, u32[]{:S(2)}, u32[]{:S(2)}) collective-permute-start(bf16[112,2048]{1,0:T(8,128)(2,1)} %collective-permute-done.10.refs_1_), channel_id=1, source_target_pairs={{0,8},{8,16},{16,24},{24,0},{1,9},{9,17},{17,25},{25,1},{2,10},{10... | collective-permute-start | bytes 1376264 | tf_op jit(solution)/shard_map/ppermute | solution.py:100
  113.2 31.1 %collective-permute-start.21 = (bf16[112,2048]{1,0:T(8,128)(2,1)}, bf16[112,2048]{1,0:T(8,128)(2,1)}, u32[]{:S(2)}, u32[]{:S(2)}) collective-permute-start(bf16[112,2048]{1,0:T(8,128)(2,1)} %collective-permute-done.14.refs_2_), channel_id=1, source_target_pairs={{0,4},{4,0},{1,5},{5,1},{2,6},{6,2},{3,7},{7,3},{8,12},{12,8},{9,1... | collective-permute-start | bytes 1376264 | tf_op jit(solution)/shard_map/ppermute | solution.py:103
  113.2 31.7 %collective-permute-start.15 = (bf16[112,2048]{1,0:T(8,128)(2,1)}, bf16[112,2048]{1,0:T(8,128)(2,1)}, u32[]{:S(2)}, u32[]{:S(2)}) collective-permute-start(bf16[112,2048]{1,0:T(8,128)(2,1)} %collective-permute-done.14.refs_2_), channel_id=1, source_target_pairs={{0,8},{8,16},{16,24},{24,0},{1,9},{9,17},{17,25},{25,1},{2,10},{10... | collective-permute-start | bytes 1376264 | tf_op jit(solution)/shard_map/ppermute | solution.py:100
  123.1 26.4 %collective-permute-start.3 = (bf16[112,2048]{1,0:T(8,128)(2,1)}, bf16[112,2048]{1,0:T(8,128)(2,1)}, u32[]{:S(2)}, u32[]{:S(2)}) collective-permute-start(bf16[112,2048]{1,0:T(8,128)(2,1)} %collective-permute-done.2.refs_3_), channel_id=1, source_target_pairs={{0,8},{8,16},{16,24},{24,0},{1,9},{9,17},{17,25},{25,1},{2,10},{10... | collective-permute-start | bytes 1376264 | tf_op jit(solution)/shard_map/ppermute | solution.py:100
  144.3 16.2 %collective-permute-start.22 = (bf16[112,2048]{1,0:T(8,128)(2,1)}, bf16[112,2048]{1,0:T(8,128)(2,1)}, u32[]{:S(2)}, u32[]{:S(2)}) collective-permute-start(bf16[112,2048]{1,0:T(8,128)(2,1)} %collective-permute-done.2.refs_3_), channel_id=1, source_target_pairs={{0,4},{4,0},{1,5},{5,1},{2,6},{6,2},{3,7},{7,3},{8,12},{12,8},{9,1... | collective-permute-start | bytes 1376264 | tf_op jit(solution)/shard_map/ppermute | solution.py:103
  144.3 20.1 %collective-permute-start.16 = (bf16[112,2048]{1,0:T(8,128)(2,1)}, bf16[112,2048]{1,0:T(8,128)(2,1)}, u32[]{:S(2)}, u32[]{:S(2)}) collective-permute-start(bf16[112,2048]{1,0:T(8,128)(2,1)} %collective-permute-done.7.refs_0_), channel_id=1, source_target_pairs={{0,4},{4,0},{1,5},{5,1},{2,6},{6,2},{3,7},{7,3},{8,12},{12,8},{9,1... | collective-permute-start | bytes 1376264 | tf_op jit(solution)/shard_map/ppermute | solution.py:103
  144.8 19.6 %collective-permute-start.17 = (bf16[112,2048]{1,0:T(8,128)(2,1)}, bf16[112,2048]{1,0:T(8,128)(2,1)}, u32[]{:S(2)}, u32[]{:S(2)}) collective-permute-start(bf16[112,2048]{1,0:T(8,128)(2,1)} %collective-permute-done.11.refs_1_), channel_id=1, source_target_pairs={{0,4},{4,0},{1,5},{5,1},{2,6},{6,2},{3,7},{7,3},{8,12},{12,8},{9,1... | collective-permute-start | bytes 1376264 | tf_op jit(solution)/shard_map/ppermute | solution.py:103
  144.9 19.6 %collective-permute-start.18 = (bf16[112,2048]{1,0:T(8,128)(2,1)}, bf16[112,2048]{1,0:T(8,128)(2,1)}, u32[]{:S(2)}, u32[]{:S(2)}) collective-permute-start(bf16[112,2048]{1,0:T(8,128)(2,1)} %collective-permute-done.15.refs_2_), channel_id=1, source_target_pairs={{0,4},{4,0},{1,5},{5,1},{2,6},{6,2},{3,7},{7,3},{8,12},{12,8},{9,1... | collective-permute-start | bytes 1376264 | tf_op jit(solution)/shard_map/ppermute | solution.py:103
  149.5 18.3 %collective-permute-start.4 = (bf16[112,2048]{1,0:T(8,128)(2,1)}, bf16[112,2048]{1,0:T(8,128)(2,1)}, u32[]{:S(2)}, u32[]{:S(2)}) collective-permute-start(bf16[112,2048]{1,0:T(8,128)(2,1)} %collective-permute-done.3.refs_0_), channel_id=1, source_target_pairs={{0,4},{4,0},{1,5},{5,1},{2,6},{6,2},{3,7},{7,3},{8,12},{12,8},{9,1... | collective-permute-start | bytes 1376264 | tf_op jit(solution)/shard_map/ppermute | solution.py:103
  (13 other events, 76.5 us)
